TPU v7x, 32 devices: a whole 2x2x4 slice. The times are simulated.
32 devices in a mesh: wide: 8 (over z, core), narrow: 4 (over y, x).
Axes of the slice: x: 2, y: 2, z: 4, core: 2. Of those that a mesh axis runs over, the one named last changes fastest.
Arguments:
- tridiag_vectors: float32 [128, 131072], P(('wide', 'narrow')), may hold values from -6 to 6
- reflectors: float32 [2, 131072, 256], P(None, 'wide'), may hold values from -0.015625 to 0.015625
- triangles: float32 [2, 256, 256], replicated, as said below
- lower_blocks: float32 [6, 1536, 1536], P(None, 'wide'), may hold values from -0.109375 to 0.109375
- diag_inverses: float32 [4, 1536, 1536], P(None, None, 'wide'), as said below
Outputs:
- transformed: float32 [128, 131072], P('narrow', 'wide')
- solved: float32 [128, 4, 1536], P('narrow', None, 'wide')
Inputs may be any that keep to these rules, and one draw needn't show every extreme that they name: `triangles`: zero below the diagonal, positive on it. `diag_inverses`: zero above the diagonal, positive on it.
All inputs are finite; a program needn't handle non-finite values.
Results may differ from a plain program's by a relative error of at most 0.00019.
Values sent between devices are 32-bit elements; how exact they have to be, the bound alone decides.
A program may use at most 128 MiB of HBM per device.

v0:
```python
import jax
import jax.numpy as jnp
from jax import lax
from jax.sharding import PartitionSpec as P

HIGHEST = lax.Precision.HIGHEST


def reflect(current, vectors, factor, products):
    coeffs = jnp.dot(products, factor.T, precision=HIGHEST)
    return current - jnp.dot(coeffs, vectors.T, precision=HIGHEST)


def add_piece(inverse, segment):
    return jnp.dot(segment, inverse, precision=HIGHEST)


def solve_chain(corner, lower_blocks, diag_inverses):
    local_count, panels, share_cols = corner.shape
    zeroed = jnp.zeros((local_count, share_cols), jnp.float32)
    pending = [zeroed] * panels
    results = [zeroed] * panels
    for source in reversed(range(panels)):
        remain = corner[:, source, :] - pending[source]
        solution = add_piece(
            diag_inverses[source], lax.all_gather(remain, "wide", axis=1, tiled=True)
        )
        results[source] = solution
        if source > 0:
            offset = source * (source - 1) // 2
            blocks = lower_blocks[offset : offset + source]
            partial_terms = jnp.einsum("ks,qsc->kqc", solution, blocks, precision=HIGHEST)
            scattered = lax.psum_scatter(partial_terms, "wide", scatter_dimension=2, tiled=True)
            for target in range(source):
                pending[target] = pending[target] + scattered[:, target, :]
    return jnp.stack(results, axis=1)


def body(tridiag_vectors, reflectors, triangles, lower_blocks, diag_inverses):
    wide_size = lax.axis_size("wide")
    spread = lax.all_to_all(
        tridiag_vectors, ("wide", "narrow"), split_axis=1, concat_axis=0, tiled=True
    )
    current = lax.all_to_all(spread, "narrow", split_axis=0, concat_axis=1, tiled=True)
    for which in (1, 0):
        products = lax.psum(jnp.dot(current, reflectors[which], precision=HIGHEST), "wide")
        current = reflect(current, reflectors[which], triangles[which], products)
    panels, panel_rows, share_cols = diag_inverses.shape
    corner_span = panels * panel_rows
    tail_cols = current[:, current.shape[1] - corner_span :]
    framed = tail_cols.reshape(tail_cols.shape[0], panels, wide_size, share_cols)
    received = lax.all_to_all(framed, "wide", split_axis=2, concat_axis=2, tiled=True)
    corner = received[:, :, wide_size - 1, :]
    solved = solve_chain(corner, lower_blocks, diag_inverses)
    return (current, solved)


def solution(mesh):
    placed = (
        P(("wide", "narrow"), None),
        P(None, "wide", None),
        P(),
        P(None, "wide", None),
        P(None, None, "wide"),
    )
    return jax.shard_map(
        body,
        mesh=mesh,
        in_specs=placed,
        out_specs=(P("narrow", "wide"), P("narrow", None, "wide")),
        check_vma=False,
    )
```

profile of v0, /device:TPU:0, one launch (start us, length us, event | category | flops | bytes accessed | tf_op | source)
XLA Modules:
  0.0 433.0 jit_solution(8765695923981802089)
XLA Ops:
  7.2 0.0 reduce-scatter.10.cloned.1.call-start
  7.2 56.5 %all_to_all.40 = f32[4,32,4096]{2,0,1:T(4,128)} all-to-all(f32[4,32,4096]{2,0,1:T(4,128)} %bitcast.93), channel_id=1, replica_groups=mesh['wide'=8,'narrow'=4] {'wide','narrow'}, dimensions={1} | all-to-all | bytes 4194304 | tf_op jit(solution)/shard_map/all_to_all | solution.py:41
  63.7 2.0 all_to_all.32
  65.6 28.2 %all_to_all.41 = f32[4,32,4096]{2,1,0:T(8,128)S(1)} all-to-all(f32[4,32,4096]{2,1,0:T(8,128)S(1)} %all_to_all.32), channel_id=1, replica_groups=mesh['wide'=8,'narrow'=4] {'narrow'}, dimensions={0} | all-to-all | bytes 4194304 | tf_op jit(solution)/shard_map/all_to_all | solution.py:44
  93.8 0.1 copy.39
  94.0 0.0 copy-start
  94.0 1.3 copy-done
  95.3 0.0 copy-start.2
  95.3 10.7 %fusion.4 = f32[32,256]{1,0:T(8,128)S(1)} fusion(f32[32,16384]{1,0:T(8,128)S(1)} %bitcast.83, f32[2,16384,256]{2,1,0:T(8,128)} %param.6), kind=kOutput, calls=%fused_computation.6 | convolution fusion | flops 1610612736 | bytes 18907136 | tf_op jit(solution)/shard_map/dot_general | solution.py:46
  106.0 26.1 %psum.14 = f32[32,256]{1,0:T(8,128)S(1)} all-reduce(f32[32,256]{1,0:T(8,128)S(1)} %fusion.4), channel_id=1, replica_groups=mesh['wide'=8,'narrow'=4] {'wide'}, use_global_device_ids=true, to_apply=%region_0.0 | all-reduce | flops 8192 | bytes 65536 | tf_op jit(solution)/shard_map/psum | solution.py:46
  132.1 0.0 copy-done.2
  132.1 0.3 fusion.33
  132.5 18.6 %convolution_subtract_fusion.1 = f32[32,16384]{1,0:T(8,128)S(1)} fusion(f32[32,16384]{1,0:T(8,128)} %bitcast.84, f32[32,256]{1,0:T(8,128)S(1)} %fusion.33, f32[2,16384,256]{2,1,0:T(8,128)} %param.6), kind=kOutput, calls=%fused_computation.1 | convolution fusion | flops 1611137024 | bytes 21004288 | tf_op jit(solution)/shard_map/dot_general | solution.py:11
  151.1 10.6 %fusion.1 = f32[32,256]{1,0:T(8,128)S(1)} fusion(f32[32,16384]{1,0:T(8,128)S(1)} %convolution_subtract_fusion.1, f32[2,16384,256]{2,1,0:T(8,128)} %param.6), kind=kOutput, calls=%fused_computation.3 | convolution fusion | flops 1610612736 | bytes 18907136 | tf_op jit(solution)/shard_map/dot_general | solution.py:46
  161.8 26.2 %psum.15 = f32[32,256]{1,0:T(8,128)S(1)} all-reduce(f32[32,256]{1,0:T(8,128)S(1)} %fusion.1), channel_id=1, replica_groups=mesh['wide'=8,'narrow'=4] {'wide'}, use_global_device_ids=true, to_apply=%region_1.0 | all-reduce | flops 8192 | bytes 65536 | tf_op jit(solution)/shard_map/psum | solution.py:46
  187.9 0.3 fusion.31
  188.3 17.3 %convolution_subtract_fusion = f32[32,16384]{1,0:T(8,128)S(1)} fusion(f32[32,16384]{1,0:T(8,128)S(1)} %convolution_subtract_fusion.1, f32[32,256]{1,0:T(8,128)S(1)} %fusion.31, f32[2,16384,256]{2,1,0:T(8,128)} %param.6), kind=kOutput, calls=%fused_computation | convolution fusion | flops 1611137024 | bytes 21004288 | tf_op jit(solution)/shard_map/dot_general | solution.py:11
  205.5 0.0 copy-start.1
  205.5 1.3 copy-done.1
  206.9 0.1 slice.90
  206.9 0.5 reshape.24
  207.4 0.6 copy.22
  208.0 29.0 %all_to_all.42 = f32[32,4,8,192]{3,0,1,2:T(8,128)S(1)} all-to-all(f32[32,4,8,192]{3,0,1,2:T(8,128)S(1)} %copy.22), channel_id=1, replica_groups=mesh['wide'=8,'narrow'=4] {'wide'}, dimensions={2} | all-to-all | bytes 1572864 | tf_op jit(solution)/shard_map/all_to_all | solution.py:52
  237.0 0.1 copy.23
  237.1 15.7 %all-gather = f32[32,1,1536]{0,1,2:T(1,128)S(1)} all-gather(f32[32,1,192]{0,1,2:T(1,128)S(1)} %copy.23), channel_id=2, replica_groups=mesh['wide'=8,'narrow'=4] {'wide'}, dimensions={2}, use_global_device_ids=true | all-gather | bytes 221184 | tf_op jit(solution)/shard_map/all_gather | solution.py:26
  252.9 2.6 fusion.21
  255.5 5.0 %fusion.10 = f32[32,3,1536]{2,0,1:T(8,128)} fusion(f32[6,192,1536]{2,1,0:T(8,128)} %param.8, f32[32,192]{1,0:T(8,128)S(1)} %fusion.21), kind=kOutput, calls=%fused_computation.12 | convolution fusion | flops 339738624 | bytes 4153344 | tf_op jit(solution)/shard_map/ks,qsc->kqc/dot_general | solution.py:32
  260.5 2.6 copy.28
  263.2 2.2 reshape.32
  265.4 0.0 reduce-scatter.10.cloned.1.call-update
  265.4 0.0 reduce-scatter.12.cloned.1.call-start
  265.5 29.5 %reduce-scatter.10.cloned.1.call-done = f32[192,96]{1,0:T(8,128)} async-done(((f32[1536,96]{1,0:T(8,128)}), f32[192,96]{1,0:T(8,128)}) %reduce-scatter.10.cloned.1.call-update) | async-done | bytes 73744
  295.0 1.1 reshape.33
  296.1 0.2 fusion.39
  296.3 0.1 copy.35
  296.4 0.1 copy.24
  296.5 16.0 %all-gather.1 = f32[32,1,1536]{0,1,2:T(1,128)S(1)} all-gather(f32[32,1,192]{0,1,2:T(1,128)S(1)} %copy.24), channel_id=3, replica_groups=mesh['wide'=8,'narrow'=4] {'wide'}, dimensions={2}, use_global_device_ids=true | all-gather | bytes 221184 | tf_op jit(solution)/shard_map/all_gather | solution.py:26
  312.5 2.6 fusion.19
  315.1 3.2 fusion.12
  318.3 0.8 copy.30
  319.1 1.8 reshape.34
  320.9 0.0 reduce-scatter.12.cloned.1.call-update
  320.9 0.0 reduce-scatter.14.cloned.1.call-start
  321.0 0.1 copy.37
  321.0 30.2 %reduce-scatter.12.cloned.1.call-done = f32[192,64]{1,0:T(8,128)} async-done(((f32[1536,64]{1,0:T(8,128)}), f32[192,64]{1,0:T(8,128)}) %reduce-scatter.12.cloned.1.call-update) | async-done | bytes 49168
  351.2 1.0 reshape.35
  352.3 0.2 fusion.40
  352.4 0.1 copy.38
  352.5 0.1 copy.25
  352.6 15.7 %all-gather.2 = f32[32,1,1536]{0,1,2:T(1,128)S(1)} all-gather(f32[32,1,192]{0,1,2:T(1,128)S(1)} %copy.25), channel_id=4, replica_groups=mesh['wide'=8,'narrow'=4] {'wide'}, dimensions={2}, use_global_device_ids=true | all-gather | bytes 221184 | tf_op jit(solution)/shard_map/all_gather | solution.py:26
  368.4 2.6 fusion.17
  371.0 4.8 %convolution_bitcast_fusion = f32[1536,32]{1,0:T(8,128)} fusion(f32[32,192]{1,0:T(8,128)S(1)} %fusion.17, f32[6,192,1536]{2,1,0:T(8,128)} %param.8), kind=kOutput, calls=%fused_computation.14 | convolution fusion | flops 113246208 | bytes 1400832 | tf_op jit(solution)/shard_map/ks,qsc->kqc/dot_general | solution.py:32
  375.8 0.0 reduce-scatter.14.cloned.1.call-update
  375.8 0.1 copy.34
  375.9 0.1 copy.36
  375.9 30.3 %reduce-scatter.14.cloned.1.call-done = f32[192,32]{1,0:T(8,128)} async-done(((f32[1536,32]{1,0:T(8,128)}), f32[192,32]{1,0:T(8,128)}) %reduce-scatter.14.cloned.1.call-update) | async-done | bytes 24592
  406.3 1.0 copy.33
  407.2 0.1 copy.26
  407.3 15.7 %all-gather.3 = f32[32,1,1536]{0,1,2:T(1,128)S(1)} all-gather(f32[32,1,192]{0,1,2:T(1,128)S(1)} %copy.26), channel_id=5, replica_groups=mesh['wide'=8,'narrow'=4] {'wide'}, dimensions={2}, use_global_device_ids=true | all-gather | bytes 221184 | tf_op jit(solution)/shard_map/all_gather | solution.py:26
  423.1 2.6 fusion.28
  425.7 0.7 copy.27
  (6 shorter events, 0.1 us)
Async XLA Ops:
  7.2 287.9 %reduce-scatter.10.cloned.1.call-start = ((), (), s32[]{:S(2)}) async-start(), calls=%async_computation.6 | async-start | bytes 884736
  94.0 1.3 copy-start
  95.3 36.8 %copy-start.2 = (f32[2,256,256]{2,1,0:T(8,128)S(1)}, f32[2,256,256]{2,1,0:T(8,128)}, u32[]{:S(2)}) copy-start(f32[2,256,256]{2,1,0:T(8,128)} %param.7) | copy-start | bytes 1572868
  205.5 1.3 copy-start.1
  265.4 85.8 %reduce-scatter.12.cloned.1.call-start = ((), (), s32[]{:S(2)}) async-start(), calls=%async_computation.7 | async-start | bytes 884736
  320.9 85.4 %reduce-scatter.14.cloned.1.call-start = ((), (), s32[]{:S(2)}) async-start(), calls=%async_computation.8 | async-start | bytes 884736
Sparse Core Ops, SparseCore 0:
  265.6 29.4 reduce-scatter.9
  321.0 30.1 reduce-scatter.11
  375.9 30.2 reduce-scatter.13
where the time goes:
time: 434 us; the launch traced here: 433 us
  blocking collectives  229 us (53%)
  waiting for transfers between devices  90.1 us (21%)
  matrix products  81.5 us (19%)
  local copies, waits for them, and re-layouts  18.2 us (4%)
  between operations  14 us (3%)
    unnamed x6, waiting for transfers between devices  90.1 us
    all_gather x4, blocking collectives, solve_chain(): lax.all_gather(remain, 'wide', axis=1, tiled=True)  63.2 us
    all_to_all x1, blocking collectives, body(): lax.all_to_all(tridiag_vectors, ('wide', 'narrow'), split_axis=1, concat_...  56.5 us
    psum x2, blocking collectives, body(): lax.psum(jnp.dot(current, reflectors[which], precision=HIGHEST), 'wide')  52.3 us
    dot_general x2, matrix products, reflect(): return current - jnp.dot(coeffs, vectors.T, precision=HIGHEST)  35.9 us
    all_to_all x1, blocking collectives, body(): lax.all_to_all(framed, 'wide', split_axis=2, concat_axis=2, tiled=True)  29 us
    all_to_all x1, blocking collectives, body(): lax.all_to_all(spread, 'narrow', split_axis=0, concat_axis=1, tiled=True)  28.2 us
    dot_general x2, matrix products, body(): jnp.dot(current, reflectors[which], precision=HIGHEST)  21.3 us
  transfers between devices with their start and end apart: 3, of which 3 were waited for; matrix products, arithmetic and copies ran while one was open for 0% of the time, Pallas kernels for 0%

commit v1 on v0

--- a/solution.py
+++ b/solution.py
@@ -23,7 +23,10 @@
     for source in reversed(range(panels)):
         remain = corner[:, source, :] - pending[source]
         solution = add_piece(
-            diag_inverses[source], lax.all_gather(remain, "wide", axis=1, tiled=True)
+            diag_inverses[source],
+            jnp.concatenate(
+                lax.all_to_all(jnp.stack([remain] * lax.axis_size("wide")), "wide", 0, 0), axis=1
+            ),
         )
         results[source] = solution
         if source > 0:

time: 434 us -> 420 us (0.968)
  blocking collectives: 229 us -> 214 us
    all_gather x4 -> x0, blocking collectives: 63.2 us -> none  [solve_chain(): lax.all_gather(remain, 'wide', axis=1, tiled=True)]
    all_to_all x0 -> x4, blocking collectives: none -> 48.5 us  [solve_chain(): lax.all_to_all(jnp.stack([remain] * lax.axis_size('wide')), 'wide', 0, 0)]
where the time goes in v1:
time: 420 us
  blocking collectives  214 us (51%)
  waiting for transfers between devices  91.3 us (22%)
  matrix products  80.7 us (19%)
  local copies, waits for them, and re-layouts  19 us (5%)
  between operations  14 us (3%)
    unnamed x6, waiting for transfers between devices  91.3 us
    all_to_all x1, blocking collectives, body(): lax.all_to_all(tridiag_vectors, ('wide', 'narrow'), split_axis=1, concat_...  56.5 us
    psum x2, blocking collectives, body(): lax.psum(jnp.dot(current, reflectors[which], precision=HIGHEST), 'wide')  52.3 us
    all_to_all x4, blocking collectives, solve_chain(): lax.all_to_all(jnp.stack([remain] * lax.axis_size('wide')), 'wide', 0, 0)  48.5 us
    dot_general x2, matrix products, reflect(): return current - jnp.dot(coeffs, vectors.T, precision=HIGHEST)  35.9 us
    all_to_all x1, blocking collectives, body(): lax.all_to_all(framed, 'wide', split_axis=2, concat_axis=2, tiled=True)  29 us
    all_to_all x1, blocking collectives, body(): lax.all_to_all(spread, 'narrow', split_axis=0, concat_axis=1, tiled=True)  28.2 us
    dot_general x2, matrix products, body(): jnp.dot(current, reflectors[which], precision=HIGHEST)  21.3 us
  transfers between devices with their start and end apart: 3, of which 3 were waited for; matrix products, arithmetic and copies ran while one was open for 0% of the time, Pallas kernels for 0%

profile of v1, /device:TPU:0, one launch (start us, length us, event | category | flops | bytes accessed | tf_op | source)
XLA Modules:
  0.0 419.6 jit_solution(17973680428649461891)
XLA Ops:
  7.2 0.0 reduce-scatter.10.cloned.1.call-start
  7.2 56.5 %all_to_all.60 = f32[4,32,4096]{2,0,1:T(4,128)} all-to-all(f32[4,32,4096]{2,0,1:T(4,128)} %bitcast.97), channel_id=1, replica_groups=mesh['wide'=8,'narrow'=4] {'wide','narrow'}, dimensions={1} | all-to-all | bytes 4194304 | tf_op jit(solution)/shard_map/all_to_all | solution.py:44
  63.7 2.0 all_to_all.44
  65.6 28.2 %all_to_all.61 = f32[4,32,4096]{2,1,0:T(8,128)S(1)} all-to-all(f32[4,32,4096]{2,1,0:T(8,128)S(1)} %all_to_all.44), channel_id=1, replica_groups=mesh['wide'=8,'narrow'=4] {'narrow'}, dimensions={0} | all-to-all | bytes 4194304 | tf_op jit(solution)/shard_map/all_to_all | solution.py:47
  93.8 0.1 copy.32
  94.0 0.0 copy-start
  94.0 1.3 copy-done
  95.3 10.7 %fusion.4 = f32[32,256]{1,0:T(8,128)S(1)} fusion(f32[32,16384]{1,0:T(8,128)S(1)} %bitcast.91, f32[2,16384,256]{2,1,0:T(8,128)} %param.6), kind=kOutput, calls=%fused_computation.6 | convolution fusion | flops 1610612736 | bytes 18907136 | tf_op jit(solution)/shard_map/dot_general | solution.py:49
  106.0 26.1 %psum.14 = f32[32,256]{1,0:T(8,128)S(1)} all-reduce(f32[32,256]{1,0:T(8,128)S(1)} %fusion.4), channel_id=1, replica_groups=mesh['wide'=8,'narrow'=4] {'wide'}, use_global_device_ids=true, to_apply=%region_0.0 | all-reduce | flops 8192 | bytes 65536 | tf_op jit(solution)/shard_map/psum | solution.py:49
  132.1 0.0 copy-done.2
  132.1 0.3 fusion.33
  132.5 18.6 %convolution_subtract_fusion.1 = f32[32,16384]{1,0:T(8,128)S(1)} fusion(f32[32,16384]{1,0:T(8,128)} %bitcast.92, f32[32,256]{1,0:T(8,128)S(1)} %fusion.33, f32[2,16384,256]{2,1,0:T(8,128)} %param.6), kind=kOutput, calls=%fused_computation.1 | convolution fusion | flops 1611137024 | bytes 21004288 | tf_op jit(solution)/shard_map/dot_general | solution.py:11
  151.1 10.6 %fusion.1 = f32[32,256]{1,0:T(8,128)S(1)} fusion(f32[32,16384]{1,0:T(8,128)S(1)} %convolution_subtract_fusion.1, f32[2,16384,256]{2,1,0:T(8,128)} %param.6), kind=kOutput, calls=%fused_computation.3 | convolution fusion | flops 1610612736 | bytes 18907136 | tf_op jit(solution)/shard_map/dot_general | solution.py:49
  161.8 26.2 %psum.15 = f32[32,256]{1,0:T(8,128)S(1)} all-reduce(f32[32,256]{1,0:T(8,128)S(1)} %fusion.1), channel_id=1, replica_groups=mesh['wide'=8,'narrow'=4] {'wide'}, use_global_device_ids=true, to_apply=%region_1.0 | all-reduce | flops 8192 | bytes 65536 | tf_op jit(solution)/shard_map/psum | solution.py:49
  187.9 0.3 fusion.31
  188.3 17.3 %convolution_subtract_fusion = f32[32,16384]{1,0:T(8,128)S(1)} fusion(f32[32,16384]{1,0:T(8,128)S(1)} %convolution_subtract_fusion.1, f32[32,256]{1,0:T(8,128)S(1)} %fusion.31, f32[2,16384,256]{2,1,0:T(8,128)} %param.6), kind=kOutput, calls=%fused_computation | convolution fusion | flops 1611137024 | bytes 21004288 | tf_op jit(solution)/shard_map/dot_general | solution.py:11
  205.5 0.0 copy-start.1
  205.5 1.3 copy-done.1
  206.9 0.1 slice.90
  206.9 0.5 reshape.71
  207.4 0.6 copy.15
  208.0 29.0 %all_to_all.62 = f32[32,4,8,192]{3,0,1,2:T(8,128)S(1)} all-to-all(f32[32,4,8,192]{3,0,1,2:T(8,128)S(1)} %copy.15), channel_id=1, replica_groups=mesh['wide'=8,'narrow'=4] {'wide'}, dimensions={2} | all-to-all | bytes 1572864 | tf_op jit(solution)/shard_map/all_to_all | solution.py:55
  237.0 12.1 %all_to_all.63 = f32[8,32,192]{2,1,0:T(8,128)S(1)} all-to-all(f32[8,32,192]{2,1,0:T(8,128)S(1)} %stack.18), channel_id=1, replica_groups=mesh['wide'=8,'narrow'=4] {'wide'}, dimensions={0} | all-to-all | bytes 393216 | tf_op jit(solution)/shard_map/all_to_all | solution.py:28
  249.2 0.2 copy.16
  249.3 0.1 reshape.73
  249.4 2.5 fusion.21
  251.9 5.0 %fusion.10 = f32[32,3,1536]{2,0,1:T(8,128)} fusion(f32[6,192,1536]{2,1,0:T(8,128)} %param.8, f32[32,192]{1,0:T(8,128)S(1)} %fusion.21), kind=kOutput, calls=%fused_computation.12 | convolution fusion | flops 339738624 | bytes 4153344 | tf_op jit(solution)/shard_map/ks,qsc->kqc/dot_general | solution.py:35
  257.0 2.6 copy.21
  259.6 2.2 reshape.83
  261.8 0.0 reduce-scatter.10.cloned.1.call-update
  261.8 0.0 reduce-scatter.12.cloned.1.call-start
  261.9 29.6 %reduce-scatter.10.cloned.1.call-done = f32[192,96]{1,0:T(8,128)} async-done(((f32[1536,96]{1,0:T(8,128)}), f32[192,96]{1,0:T(8,128)}) %reduce-scatter.10.cloned.1.call-update) | async-done | bytes 73744
  291.4 1.1 reshape.84
  292.5 0.2 fusion.42
  292.7 0.1 copy.28
  292.9 12.1 %all_to_all.64 = f32[8,32,192]{2,1,0:T(8,128)S(1)} all-to-all(f32[8,32,192]{2,1,0:T(8,128)S(1)} %stack.19), channel_id=1, replica_groups=mesh['wide'=8,'narrow'=4] {'wide'}, dimensions={0} | all-to-all | bytes 393216 | tf_op jit(solution)/shard_map/all_to_all | solution.py:28
  305.0 0.2 copy.17
  305.1 0.1 reshape.75
  305.3 2.5 fusion.19
  307.7 3.2 fusion.12
  310.9 0.8 copy.23
  311.7 1.8 reshape.85
  313.5 0.0 reduce-scatter.12.cloned.1.call-update
  313.5 0.0 reduce-scatter.14.cloned.1.call-start
  313.5 0.1 copy.30
  313.6 30.8 %reduce-scatter.12.cloned.1.call-done = f32[192,64]{1,0:T(8,128)} async-done(((f32[1536,64]{1,0:T(8,128)}), f32[192,64]{1,0:T(8,128)}) %reduce-scatter.12.cloned.1.call-update) | async-done | bytes 49168
  344.4 1.0 reshape.86
  345.5 0.2 fusion.43
  345.6 0.1 copy.31
  345.7 12.1 %all_to_all.65 = f32[8,32,192]{2,1,0:T(8,128)S(1)} all-to-all(f32[8,32,192]{2,1,0:T(8,128)S(1)} %stack.20), channel_id=1, replica_groups=mesh['wide'=8,'narrow'=4] {'wide'}, dimensions={0} | all-to-all | bytes 393216 | tf_op jit(solution)/shard_map/all_to_all | solution.py:28
  357.9 0.2 copy.18
  358.0 0.1 reshape.77
  358.1 2.5 fusion.17
  360.6 4.8 %convolution_bitcast_fusion = f32[1536,32]{1,0:T(8,128)} fusion(f32[32,192]{1,0:T(8,128)S(1)} %fusion.17, f32[6,192,1536]{2,1,0:T(8,128)} %param.8), kind=kOutput, calls=%fused_computation.14 | convolution fusion | flops 113246208 | bytes 1400832 | tf_op jit(solution)/shard_map/ks,qsc->kqc/dot_general | solution.py:35
  365.4 0.0 reduce-scatter.14.cloned.1.call-update
  365.4 0.1 copy.27
  365.5 0.1 copy.29
  365.5 30.9 %reduce-scatter.14.cloned.1.call-done = f32[192,32]{1,0:T(8,128)} async-done(((f32[1536,32]{1,0:T(8,128)}), f32[192,32]{1,0:T(8,128)}) %reduce-scatter.14.cloned.1.call-update) | async-done | bytes 24592
  396.4 1.0 copy.26
  397.4 12.1 %all_to_all.66 = f32[8,32,192]{2,1,0:T(8,128)S(1)} all-to-all(f32[8,32,192]{2,1,0:T(8,128)S(1)} %stack.21), channel_id=1, replica_groups=mesh['wide'=8,'narrow'=4] {'wide'}, dimensions={0} | all-to-all | bytes 393216 | tf_op jit(solution)/shard_map/all_to_all | solution.py:28
  409.5 0.2 copy.19
  409.7 0.1 reshape.80
  409.8 2.4 fusion.28
  412.3 0.7 copy.20
  (11 shorter events, 0.2 us)
Async XLA Ops:
  7.2 284.3 %reduce-scatter.10.cloned.1.call-start = ((), (), s32[]{:S(2)}) async-start(), calls=%async_computation.10 | async-start | bytes 884736
  94.0 1.3 copy-start
  95.3 36.8 %copy-start.2 = (f32[2,256,256]{2,1,0:T(8,128)S(1)}, f32[2,256,256]{2,1,0:T(8,128)}, u32[]{:S(2)}) copy-start(f32[2,256,256]{2,1,0:T(8,128)} %param.7) | copy-start | bytes 1572868
  205.5 1.3 copy-start.1
  261.8 82.6 %reduce-scatter.12.cloned.1.call-start = ((), (), s32[]{:S(2)}) async-start(), calls=%async_computation.11 | async-start | bytes 884736
  313.5 82.9 %reduce-scatter.14.cloned.1.call-start = ((), (), s32[]{:S(2)}) async-start(), calls=%async_computation.12 | async-start | bytes 884736
Sparse Core Ops, SparseCore 0:
  262.0 29.4 reduce-scatter.9
  313.6 30.7 reduce-scatter.11
  365.5 30.8 reduce-scatter.13
